TPU v7x, 32 devices: a whole 2x2x4 slice. The times are simulated.
32 devices in a mesh: seq: 8 (over z, y), head: 4 (over x, core).
Axes of the slice: x: 2, y: 2, z: 4, core: 2. Of those that a mesh axis runs over, the one named last changes fastest.
Arguments:
- queries: bfloat16 [1024, 4096], P('seq', 'head'), may hold values from -40 to 40
- keys: bfloat16 [1024, 512], P(('seq', 'head')), may hold values from -40 to 40
- values: bfloat16 [1024, 512], P(('seq', 'head')), may hold values from -6 to 6
- block_order: int32 [8], replicated, may hold values from 0 to 7, each once
Outputs:
- attended: bfloat16 [1024, 4096], P('seq', 'head')
All inputs are finite; a program needn't handle non-finite values.
Results may differ from a plain program's by a relative error of at most 0.0055.
Values may be sent and summed in bfloat16 or wider, within the bound.
A program may use at most 64 MiB of HBM per device.

v0:
```python
import functools
import math

import jax
import jax.numpy as jnp
from jax import lax
from jax.experimental import pallas as pl
from jax.experimental.pallas import tpu as pltpu
from jax.sharding import PartitionSpec as P

HD = 128
NEG = -1e30
MESH = pl.DeviceIdType.MESH


def kernel(
    outer, inner, heads,
    order, q_hbm, k_hbm, v_hbm, acc, total,
    q_ref, k_ref, v_ref, kz, vz, kd, vd, high,
    load_sem, own_sem, zsend, zrecv, psend, precv,
):
    rows, _ = k_ref.shape
    block = q_ref.shape[0]
    width = kd.shape[-1]
    q_heads = q_ref.shape[1] // HD
    seq, head = lax.axis_index("seq"), lax.axis_index("head")
    o, j = seq // inner, lax.rem(seq, inner)
    power = outer & (outer - 1) == 0

    bits = [1 << i for i in range(outer.bit_length() - 1)] if power else range(1, outer)

    def source(k):
        return jnp.bitwise_xor(o, k) if power else lax.rem(o - k + outer, outer)

    def target(k):
        return jnp.bitwise_xor(o, k) if power else lax.rem(o + k, outer)

    loads = [
        pltpu.make_async_copy(src, dst, load_sem.at[i])
        for i, (src, dst) in enumerate(((k_hbm, k_ref), (v_hbm, v_ref), (q_hbm, q_ref)))
    ]
    for load in loads:
        load.start()

    group = [(dj, dh) for dj in range(inner) for dh in range(heads)]

    def member(dj, dh):
        return lax.rem(j + dj, inner), lax.rem(head + dh, heads)

    barrier = pltpu.get_barrier_semaphore()
    for dj, dh in group[1:]:
        j2, h2 = member(dj, dh)
        pl.semaphore_signal(barrier, inc=1, device_id=(o * inner + j2, h2), device_id_type=MESH)

    for k in bits:
        pl.semaphore_signal(
            barrier, inc=1, device_id=(target(k) * inner + j, head), device_id_type=MESH
        )

    def steps(first, last, body):
        if last - first <= 8:
            for k in range(first, last):
                body(k, 0)
        else:
            lax.fori_loop(first, last, body, 0)

    pl.semaphore_wait(barrier, len(group) - 1 + len(bits))
    loads[0].wait()
    loads[1].wait()

    def zcopy(piece, k, bit, which):
        return pltpu.make_async_remote_copy(
            src_ref=piece,
            dst_ref=(kz, vz)[which].at[k - 1],
            send_sem=zsend.at[which],
            recv_sem=zrecv.at[k, which],
            device_id=(target(bit) * inner + j, head),
            device_id_type=MESH,
        )

    def forward(piece, k, which):
        for bit in bits:
            if isinstance(k, int):
                if bit < k & -k:
                    zcopy(piece, k + bit, bit, which).start()
            else:

                @pl.when(bit < (k & -k))
                def _(bit=bit):
                    zcopy(piece, k + bit, bit, which).start()

    def scatter(piece, k, which):
        dst = (kd, vd)[which]
        place = pl.ds(pl.multiple_of(j * block + head * rows, rows), rows)
        for dj, dh in group[::-1]:
            j2, h2 = member(dj, dh)
            src = piece.at[:, pl.ds(pl.multiple_of(h2 * width, width), width)]
            if dj == 0 and dh == 0:
                pltpu.make_async_copy(src, dst.at[k, place], own_sem.at[k, which]).start()
            else:
                pltpu.make_async_remote_copy(
                    src_ref=src,
                    dst_ref=dst.at[k, place],
                    send_sem=psend.at[k, which],
                    recv_sem=precv.at[k, which],
                    device_id=(o * inner + j2, h2),
                    device_id_type=MESH,
                ).start()

    others = pl.ds(0, (len(group) - 1) * rows)

    def landed(k, which):
        dst = (kd, vd)[which].at[k, others]
        pltpu.make_async_copy(dst, dst, precv.at[k, which]).wait()
        dst = (kd, vd)[which].at[k, pl.ds(0, rows)]
        pltpu.make_async_copy(dst, dst, own_sem.at[k, which]).wait()

    def relay(k, c=0):
        for which in range(2):
            piece = (kz, vz)[which].at[k - 1]
            zcopy(piece, k, bits[0], which).wait_recv()
            if power:
                forward(piece, k, which)
            scatter(piece, k, which)
        return c

    mine = order[seq]
    factor = math.log2(math.e) / math.sqrt(HD)
    per = 2 if q_heads % 2 == 0 else 1
    lanes = per * block
    count = inner * block

    def absorb(k, first):
        src = source(k) * inner
        row = lax.broadcasted_iota(jnp.int32, (count, lanes), 0)
        col = lax.broadcasted_iota(jnp.int32, (count, lanes), 1)
        start = jnp.full((count, lanes), order[src], jnp.int32) * block
        for jj in range(1, inner):
            start = jnp.where(row >= jj * block, order[src + jj] * block - jj * block, start)
        visible = mine * block + lax.rem(col, block) >= start + row
        landed(k, 0)
        key = kd[k]
        for c in range(q_heads // per):
            q = jnp.concatenate(
                [q_ref[:, (c * per + i) * HD : (c * per + i + 1) * HD] for i in range(per)], axis=0
            )
            s = lax.dot_general(
                key, q, (((1,), (1,)), ((), ())), preferred_element_type=jnp.float32
            )
            s = jnp.where(visible, s * factor, NEG)
            at = slice(c * lanes, (c + 1) * lanes)
            top = jnp.max(s, axis=0, keepdims=True)
            if not first:
                old = high[:, at]
                top = jnp.maximum(old, top)
            p = jnp.exp2(s - top)
            high[:, at] = top
            t = jnp.sum(p, axis=0, keepdims=True)
            if c == 0:
                landed(k, 1)
                value = vd[k]
            pv = lax.dot_general(
                value,
                p.astype(jnp.bfloat16),
                (((0,), (0,)), ((), ())),
                preferred_element_type=jnp.float32,
            )
            if first:
                total[:, at] = t
                acc[:, at] = pv
            else:
                scale = jnp.exp2(old - top)
                total[:, at] = total[:, at] * scale + t
                acc[:, at] = acc[:, at] * scale + pv

    for bit in bits[::-1]:
        for which in range(2):
            zcopy((k_ref, v_ref)[which], bit, bit, which).start()
    for which in range(2):
        scatter((k_ref, v_ref)[which], 0, which)
    loads[2].wait()
    if outer <= 8:
        turn = sorted(range(outer), key=lambda k: [k >> i & 1 for i in range(outer)])
        ahead = min(2, outer - 1)
        for k in turn[1 : ahead + 1]:
            relay(k)
        for i, k in enumerate(turn):
            if 0 < i and i + ahead < outer:
                relay(turn[i + ahead])
            absorb(k, i == 0)
    else:
        absorb(0, True)

        def later(k, c):
            relay(k)
            absorb(k, False)
            return c

        lax.fori_loop(1, outer, later, 0)

    if outer > 1:
        for which in range(2):
            sent = (kz, vz)[which]
            pltpu.make_async_copy(sent, sent, zsend.at[which]).wait()

    def drain(k, c):
        for which in range(2):
            dst = (kd, vd)[which].at[k, others]
            pltpu.make_async_copy(dst, dst, psend.at[k, which]).wait()
        return c

    steps(0, outer, drain)


def finish(acc, total, out_ref):
    block, q_cols = out_ref.shape
    for g in range(q_cols // HD):
        lane = slice(g * block, (g + 1) * block)
        part = acc[:, lane] / total[:, lane]
        out_ref[:, g * HD : (g + 1) * HD] = part.T.astype(out_ref.dtype)


def local(devices, heads, queries, keys, values, block_order):
    inner = 2 if devices % 2 == 0 else 1
    outer = devices // inner
    rows, cols = keys.shape
    block, q_cols = queries.shape
    width = cols // heads
    assert width == HD and rows * heads == block
    bf16, f32 = jnp.bfloat16, jnp.float32
    far = max(outer - 1, 1)
    lanes = q_cols // HD * block
    acc, total = pl.pallas_call(
        functools.partial(kernel, outer, inner, heads),
        out_shape=(
            pltpu.VMEM((HD, lanes), f32),
            pltpu.VMEM((1, lanes), f32),
        ),
        in_specs=[pl.BlockSpec(memory_space=pltpu.SMEM)]
        + [pl.BlockSpec(memory_space=pltpu.HBM)] * 3,
        out_specs=[pl.BlockSpec(memory_space=pltpu.VMEM)] * 2,
        scratch_shapes=[
            pltpu.VMEM((block, q_cols), bf16),
            pltpu.VMEM((rows, cols), bf16),
            pltpu.VMEM((rows, cols), bf16),
            pltpu.VMEM((far, rows, cols), bf16),
            pltpu.VMEM((far, rows, cols), bf16),
            pltpu.VMEM((outer, inner * block, width), bf16),
            pltpu.VMEM((outer, inner * block, width), bf16),
            pltpu.VMEM((1, lanes), f32),
            pltpu.SemaphoreType.DMA((3,)),
            pltpu.SemaphoreType.DMA((outer, 2)),
            pltpu.SemaphoreType.DMA((2,)),
            pltpu.SemaphoreType.DMA((outer, 2)),
            pltpu.SemaphoreType.DMA((outer, 2)),
            pltpu.SemaphoreType.DMA((outer, 2)),
        ],
        compiler_params=pltpu.CompilerParams(
            collective_id=0, has_side_effects=True, vmem_limit_bytes=67043328 - 600 * 1024
        ),
    )(block_order, queries, keys, values)
    return pl.pallas_call(
        finish,
        out_shape=jax.ShapeDtypeStruct((block, q_cols), queries.dtype),
        in_specs=[pl.BlockSpec(memory_space=pltpu.VMEM)] * 2,
        out_specs=pl.BlockSpec(memory_space=pltpu.VMEM),
        compiler_params=pltpu.CompilerParams(vmem_limit_bytes=8 * 1024 * 1024),
    )(acc, total)


def solution(mesh):
    placed = (P("seq", "head"), P(("seq", "head"), None), P(("seq", "head"), None), P())
    return jax.shard_map(
        functools.partial(local, mesh.shape["seq"], mesh.shape["head"]),
        mesh=mesh, in_specs=placed, out_specs=P("seq", "head"), check_vma=False,
    )
```

profile of v0, /device:TPU:0, one launch (start us, length us, event | category | flops | bytes accessed | tf_op | source)
XLA Modules:
  0.0 18.9 jit_solution(14624667525030326189)
XLA Ops:
  0.0 18.1 %shard_map.46 = (f32[128,1024]{1,0:T(8,128)S(1)}, f32[1,1024]{1,0:T(1,128)S(1)}) custom-call(s32[8]{0:T(128)} %order.1, bf16[128,1024]{1,0:T(8,128)(2,1)} %q_hbm.1, bf16[32,512]{1,0:T(8,128)(2,1)} %k_hbm.1, bf16[32,512]{1,0:T(8,128)(2,1)} %v_hbm.1), custom_call_target="tpu_custom_call" | custom-call | tf_op jit(solution)/shard_map/pallas_call | solution.py:233
  18.1 0.8 %shard_map.47 = bf16[128,1024]{1,0:T(8,128)(2,1)} custom-call(f32[128,1024]{1,0:T(8,128)S(1)} %get-tuple-element.7.acc, f32[1,1024]{1,0:T(1,128)S(1)} %get-tuple-element.8.total), custom_call_target="tpu_custom_call" | custom-call | tf_op jit(solution)/shard_map/pallas_call | solution.py:262
where the time goes:
time: 19.1 us; the launch traced here: 18.9 us
  Pallas kernels  18.9 us (99%)
    pallas_call x1, Pallas kernels, local(): pl.pallas_call(functools.partial(kernel, outer, inner, heads), out_shape=...  18.1 us
    pallas_call x1, Pallas kernels, local(): pl.pallas_call(finish, out_shape=jax.ShapeDtypeStruct((block, q_cols), qu...  0.85 us

commit v1 on v0

v1 whole, which is shorter than its diff:
```python
import functools
import math

import jax
import jax.numpy as jnp
from jax import lax
from jax.experimental import pallas as pl
from jax.experimental.pallas import tpu as pltpu
from jax.sharding import PartitionSpec as P

HD = 128
NEG = -1e30
MESH = pl.DeviceIdType.MESH
DD=9
LAST=[0,2,1]
HORD=0
SPLIT=2


def kernel(
    outer, inner, heads,
    order_hbm, q_hbm, k_hbm, v_hbm, acc, total,
    order, q_ref, kvd, high,
    load_sem, ready, near, sent, recv,
):
    rows = k_hbm.shape[0]
    block = q_ref.shape[0]
    width = kvd.shape[-1]
    q_heads = q_ref.shape[1] // HD
    seq, head = lax.axis_index("seq"), lax.axis_index("head")
    o, j = seq // inner, lax.rem(seq, inner)
    place = pl.ds(pl.multiple_of(head * rows, rows), rows)
    far = min(DD, outer)
    halves = SPLIT
    per_half = heads // halves
    chunk = rows * per_half
    mine_half = head // per_half

    def order_of(t):
        if HORD == 0:
            return t
        if HORD == 1:
            return lax.rem(head + t, heads)
        if HORD == 2:
            return jnp.bitwise_xor(head, t)
        if HORD == 3:
            return jnp.bitwise_xor(head, heads - 1 - t)

    def loop(first, last, body):
        lax.fori_loop(first, last, lambda k, c: (body(k), c)[1], 0)

    def columns(h):
        return pl.ds(pl.multiple_of(h * width, width), width)

    def lane(dj):
        return lax.rem(j + dj, inner)

    def signal(sem, o2, j2, h2):
        pl.semaphore_signal(sem, inc=1, device_id=(o2 * inner + j2, h2), device_id_type=MESH)

    under, above = (0, o), (o + 1, outer)
    deep, high_up = (0, jnp.maximum(o - far + 1, 0)), (jnp.minimum(o + far, outer), outer)
    spot, spots = j * heads + head, inner * heads

    barrier = pltpu.get_barrier_semaphore()

    def greet(dj):
        def body(o2):
            for h2 in range(heads):
                signal(barrier, o2, lane(dj), h2)
        return body

    loop(spot + 1, spots, lambda t: signal(barrier, o, t // heads, lax.rem(t, heads)))
    loop(*above, greet(0))
    for dj in range(1, inner):
        loop(*high_up, greet(dj))
    own = [
        pltpu.make_async_copy(src.at[:, columns(head)], kvd.at[o, j, i, place], load_sem.at[0])
        for i, src in enumerate((k_hbm, v_hbm))
    ]
    qload = pltpu.make_async_copy(q_hbm, q_ref, load_sem.at[1])
    oload = pltpu.make_async_copy(order_hbm, order, load_sem.at[2])
    for c in own + [qload, oload]:
        c.start()

    ahead = spot + o * heads + deep[1] * (inner - 1) * heads
    pl.when(ahead > 0)(lambda: pl.semaphore_wait(barrier, ahead))

    def piece(o2, j2, h2):
        for i, src in enumerate((k_hbm, v_hbm)):
            pltpu.make_async_remote_copy(
                src_ref=src.at[:, columns(h2)],
                dst_ref=kvd.at[o, j, i, place],
                send_sem=sent.at[o2],
                recv_sem=recv.at[o, j, mine_half],
                device_id=(o2 * inner + j2, h2),
                device_id_type=MESH,
            ).start()

    def push(dj):
        def body(o2):
            for t in range(heads):
                piece(o2, lane(dj), order_of(t))
        return body

    def tell(dj):
        def body(o2):
            for h2 in range(heads):
                signal(ready.at[o], o2, lane(dj), h2)
        return body

    for dj in range(1, inner):
        loop(*deep, push(dj))
    loop(*under, push(0))
    loop(0, spot, lambda t: piece(o, t // heads, lax.rem(t, heads)))
    loop(0, spot, lambda t: signal(near.at[j], o, t // heads, lax.rem(t, heads)))
    for dj in range(1, inner):
        loop(*deep, tell(dj))
    loop(*under, tell(0))

    def neighbours(j2):
        first = jnp.maximum(spot + 1 - j2 * heads, 0)
        pl.when(first < heads)(lambda: pl.semaphore_wait(near.at[j2], heads - first))
        loop(first, heads, lambda h2: piece(o, j2, h2))

    loop(j, inner, neighbours)

    def upward(o2):
        wide = jnp.minimum(jnp.maximum(o2 - o - far + 1, 0), 1) * (inner - 1) + 1
        pl.semaphore_wait(ready.at[o2], wide * heads)

        def lanes_of(dj):
            for t in range(heads):
                piece(o2, lane(dj), order_of(t))

        loop(0, wide, lanes_of)

    loop(*above, upward)

    mine_part = kvd.at[0, 0, :, pl.ds(0, rows)]
    whole = kvd.at[0, 0, :, pl.ds(0, chunk)]
    part = kvd.at[0, 0, :, pl.ds(0, chunk - rows)]

    def other_half(f):
        return lax.rem(mine_half + f, halves)

    def landed(src, dj):
        for f in range(halves):
            pltpu.make_async_copy(whole, whole, recv.at[src, lane(dj), other_half(f)]).wait()

    def relay(src):
        for f in range(halves):
            part_of = other_half(f)
            pltpu.make_async_copy(whole, whole, recv.at[src, j, part_of]).wait()
            piece_of = kvd.at[src, j, :, pl.ds(pl.multiple_of(part_of * chunk, chunk), chunk)]

            def pass_on(dj, piece_of=piece_of, part_of=part_of):
                pltpu.make_async_remote_copy(
                    src_ref=piece_of,
                    dst_ref=piece_of,
                    send_sem=sent.at[src],
                    recv_sem=recv.at[src, j, part_of],
                    device_id=(o * inner + lane(dj), head),
                    device_id_type=MESH,
                ).start()

            pl.when(jnp.abs(src - o) < far)(lambda: [pass_on(dj) for dj in range(1, inner)] and None)

    half = max(outer // 2, 1)
    turned = jnp.minimum(o // half, 1)
    seen_from = o + turned * (outer - 1 - 2 * o)

    def source(i):
        a = i + (i + outer - seen_from) // outer
        return a + turned * (outer - 1 - 2 * a)

    factor = math.log2(math.e) / math.sqrt(HD)
    per = 2 if q_heads % 2 == 0 else 1
    lanes = per * block

    def absorb(src, dj, first=False):
        l = lane(dj)
        if first:
            row = lax.broadcasted_iota(jnp.int32, (block, lanes), 0)
            col = lax.broadcasted_iota(jnp.int32, (block, lanes), 1)
            visible = lax.rem(col, block) >= row
        else:
            seen = jnp.full((1, lanes), order[src * inner + l], jnp.int32) < order[seq]
        key = kvd[src, l, 0]
        value = kvd[src, l, 1]
        for c in range(q_heads // per):
            q = jnp.concatenate(
                [q_ref[:, (c * per + i) * HD : (c * per + i + 1) * HD] for i in range(per)], axis=0
            )
            s = lax.dot_general(key, q, (((1,), (1,)), ((), ())), preferred_element_type=jnp.float32)
            s = s * factor
            if first:
                s = jnp.where(visible, s, NEG)
            cols = slice(c * lanes, (c + 1) * lanes)
            top = jnp.max(s, axis=0, keepdims=True)
            if first:
                p = jnp.exp2(s - top)
                high[:, cols] = top
            else:
                old = high[:, cols]
                top = jnp.where(seen, jnp.maximum(old, top), old)
                p = jnp.exp2(s - jnp.where(seen, top, -NEG))
                high[:, cols] = top
            t = jnp.sum(p, axis=0, keepdims=True)
            pv = lax.dot_general(
                value, p.astype(jnp.bfloat16), (((0,), (0,)), ((), ())), preferred_element_type=jnp.float32
            )
            if first:
                total[:, cols] = t
                acc[:, cols] = pv
            else:
                scale = jnp.exp2(old - top)
                total[:, cols] = total[:, cols] * scale + t
                acc[:, cols] = acc[:, cols] * scale + pv

    qload.wait()
    oload.wait()
    pltpu.make_async_copy(mine_part, mine_part, load_sem.at[0]).wait()
    pltpu.make_async_copy(part, part, recv.at[o, j, mine_half]).wait()
    for f in range(1, halves):
        pltpu.make_async_copy(whole, whole, recv.at[o, j, other_half(f)]).wait()
    absorb(o, 0, True)

    def across(src):
        for dj in range(1, inner):
            landed(src, dj)
            absorb(src, dj)

    if outer == 1:
        across(o)
    elif outer <= 8:
        srcs = [source(i) for i in range(outer - 1)]
        relay(srcs[0])
        across(o)
        absorb(srcs[0], 0)
        for src in srcs[1:]:
            relay(src)
            absorb(src, 0)
        for i in LAST if outer == 4 else range(outer - 1):
            across(srcs[i])
    else:
        across(o)

        def further(i):
            src = source(i)
            relay(src)
            absorb(src, 0)
            across(src)

        loop(0, outer - 1, further)

    most = kvd.at[0, :, :, pl.ds(0, block - block // spots)]
    full = kvd.at[0]

    def drain(o2):
        pltpu.make_async_copy(full, full, sent.at[o2]).wait()

    loop(0, o, drain)
    pltpu.make_async_copy(most, most, sent.at[o]).wait()
    loop(o + 1, outer, drain)


def finish(acc, total, out_ref):
    block, q_cols = out_ref.shape
    for g in range(q_cols // HD):
        lane = slice(g * block, (g + 1) * block)
        part = acc[:, lane] / total[:, lane]
        out_ref[:, g * HD : (g + 1) * HD] = part.T.astype(out_ref.dtype)


def local(devices, heads, queries, keys, values, block_order):
    inner = 2 if devices % 2 == 0 else 1
    outer = devices // inner
    rows, cols = keys.shape
    block, q_cols = queries.shape
    width = cols // heads
    assert width == HD and rows * heads == block
    bf16, f32 = jnp.bfloat16, jnp.float32
    lanes = q_cols // HD * block
    acc, total = pl.pallas_call(
        functools.partial(kernel, outer, inner, heads),
        out_shape=(
            pltpu.VMEM((HD, lanes), f32),
            pltpu.VMEM((1, lanes), f32),
        ),
        in_specs=[pl.BlockSpec(memory_space=pltpu.HBM)] * 4,
        out_specs=[pl.BlockSpec(memory_space=pltpu.VMEM)] * 2,
        scratch_shapes=[
            pltpu.SMEM(block_order.shape, jnp.int32),
            pltpu.VMEM((block, q_cols), bf16),
            pltpu.VMEM((outer, inner, 2, block, width), bf16),
            pltpu.VMEM((1, lanes), f32),
            pltpu.SemaphoreType.DMA((3,)),
            pltpu.SemaphoreType.REGULAR((outer,)),
            pltpu.SemaphoreType.REGULAR((inner,)),
            pltpu.SemaphoreType.DMA((outer,)),
            pltpu.SemaphoreType.DMA((outer, inner, SPLIT)),
        ],
        compiler_params=pltpu.CompilerParams(
            collective_id=0, has_side_effects=True, vmem_limit_bytes=67043328 - 600 * 1024
        ),
    )(block_order, queries, keys, values)
    return pl.pallas_call(
        finish,
        out_shape=jax.ShapeDtypeStruct((block, q_cols), queries.dtype),
        in_specs=[pl.BlockSpec(memory_space=pltpu.VMEM)] * 2,
        out_specs=pl.BlockSpec(memory_space=pltpu.VMEM),
        compiler_params=pltpu.CompilerParams(vmem_limit_bytes=8 * 1024 * 1024),
    )(acc, total)


def solution(mesh):
    placed = (P("seq", "head"), P(("seq", "head"), None), P(("seq", "head"), None), P())
    return jax.shard_map(
        functools.partial(local, mesh.shape["seq"], mesh.shape["head"]),
        mesh=mesh, in_specs=placed, out_specs=P("seq", "head"), check_vma=False,
    )
```

time: 19.1 us -> 17.8 us (0.932)
  the two profiles are of different devices: /device:TPU:0 before, /device:TPU:26 now
where the time goes in v1:
time: 17.8 us; the launch traced here: 17.6 us
  Pallas kernels  17.6 us (99%)
    pallas_call x1, Pallas kernels, local(): pl.pallas_call(functools.partial(kernel, outer, inner, heads), out_shape=...  16.8 us
    pallas_call x1, Pallas kernels, local(): pl.pallas_call(finish, out_shape=jax.ShapeDtypeStruct((block, q_cols), qu...  0.85 us

profile of v1, /device:TPU:26, one launch (start us, length us, event | category | flops | bytes accessed | tf_op | source)
XLA Modules:
  0.0 17.6 jit_solution(4773898747310160091)
XLA Ops:
  0.0 16.8 %shard_map.46 = (f32[128,1024]{1,0:T(8,128)S(1)}, f32[1,1024]{1,0:T(1,128)S(1)}) custom-call(s32[8]{0:T(128)} %order_hbm.1, bf16[128,1024]{1,0:T(8,128)(2,1)} %q_hbm.1, bf16[32,512]{1,0:T(8,128)(2,1)} %k_hbm.1, bf16[32,512]{1,0:T(8,128)(2,1)} %v_hbm.1), custom_call_target="tpu_custom_call" | custom-call | tf_op jit(solution)/shard_map/pallas_call | solution.py:285
  16.8 0.8 %shard_map.47 = bf16[128,1024]{1,0:T(8,128)(2,1)} custom-call(f32[128,1024]{1,0:T(8,128)S(1)} %get-tuple-element.7.acc, f32[1,1024]{1,0:T(1,128)S(1)} %get-tuple-element.8.total), custom_call_target="tpu_custom_call" | custom-call | tf_op jit(solution)/shard_map/pallas_call | solution.py:308

commit v2 on v1

v2 whole, which is shorter than its diff:
```python
import functools
import math

import jax
import jax.numpy as jnp
from jax import lax
from jax.experimental import pallas as pl
from jax.experimental.pallas import tpu as pltpu
from jax.sharding import PartitionSpec as P

HD = 128
NEG = -1e30
MESH = pl.DeviceIdType.MESH
DD=9
ABS=True
PRIO=True
LATE=True
KB=600
NEARFIRST=True


FACTOR = math.log2(math.e) / math.sqrt(HD)


def attend(q, key, value, mask, old):
    s = lax.dot_general(key, q, (((1,), (1,)), ((), ())), preferred_element_type=jnp.float32)
    s = s * FACTOR
    if old is None:
        s = jnp.where(mask, s, NEG)
        top = jnp.max(s, axis=0, keepdims=True)
        p = jnp.exp2(s - top)
    else:
        block = s.shape[0] // len(mask)
        parts = [s[n * block : (n + 1) * block] for n in range(len(mask))]
        top = old[0]
        for part, shown in zip(parts, mask):
            top = jnp.where(shown, jnp.maximum(top, jnp.max(part, axis=0, keepdims=True)), top)
        p = jnp.concatenate(
            [jnp.exp2(part - jnp.where(shown, top, -NEG)) for part, shown in zip(parts, mask)]
        )
    t = jnp.sum(p, axis=0, keepdims=True)
    pv = lax.dot_general(
        value, p.astype(jnp.bfloat16), (((0,), (0,)), ((), ())), preferred_element_type=jnp.float32
    )
    if old is None:
        return top, t, pv
    scale = jnp.exp2(old[0] - top)
    return top, old[1] * scale + t, old[2] * scale + pv


def kernel(
    outer, inner, heads,
    order_hbm, q_hbm, k_hbm, v_hbm, acc, total,
    order, q_ref, kz, kvd, high,
    load_sem, ready, near, zsent, zrecv, dsent, sent, recv,
):
    rows, cols = k_hbm.shape
    block = q_ref.shape[0]
    width = kvd.shape[-1]
    q_heads = q_ref.shape[1] // HD
    seq, head = lax.axis_index("seq"), lax.axis_index("head")
    o, j = seq // inner, lax.rem(seq, inner)
    first_heads = max(heads // 2, 1)
    spots = inner * heads
    corner = (j == 0) & (head < first_heads)
    place = pl.ds(pl.multiple_of(j * block + head * rows, rows), rows)
    inputs = (k_hbm, v_hbm)

    def loop(first, last, body):
        lax.fori_loop(first, last, lambda k, c: (body(k), c)[1], 0)

    def columns(h):
        return pl.ds(pl.multiple_of(h * width, width), width)

    def lane(dj):
        return lax.rem(j + dj, inner)

    def signal(sem, o2, j2, h2):
        pl.semaphore_signal(sem, inc=1, device_id=(o2 * inner + j2, h2), device_id_type=MESH)

    barrier = pltpu.get_barrier_semaphore()

    def each_spot(js, hs, sem):
        def row(j2):
            def one(h2):
                pl.when((j2 != j) | (h2 != head))(lambda: signal(sem, o, j2, h2))
            loop(*hs, one)
        loop(*js, row)

    loop(o + 1, outer, lambda o2: signal(barrier, o2, j, head))
    each_spot((j, inner), (head, heads), barrier)

    @pl.when(corner & (o == 0))
    def _():
        def row(o2):
            for j2 in range(inner):
                for h2 in range(heads):
                    pl.when((j2 != j) | (h2 != head))(lambda: signal(barrier, o2, j2, h2))

        loop(DD, outer, row)

    own = [
        pltpu.make_async_copy(src.at[:, columns(head)], kvd.at[o, i, place], load_sem.at[0])
        for i, src in enumerate(inputs)
    ]
    qload = pltpu.make_async_copy(q_hbm, q_ref, load_sem.at[1])
    oload = pltpu.make_async_copy(order_hbm, order, load_sem.at[2])
    for c in own + [qload, oload]:
        c.start()

    ahead = o + (j + 1) * (head + 1) - 1
    extra = first_heads - jnp.where(corner, 1, 0)
    ahead = ahead + jnp.where(o >= DD, extra, 0)
    pl.when(ahead > 0)(lambda: pl.semaphore_wait(barrier, ahead))

    def zsend(o2):
        for i, src in enumerate(inputs):
            pltpu.make_async_remote_copy(
                src_ref=src,
                dst_ref=kz.at[o, i],
                send_sem=zsent.at[0],
                recv_sem=zrecv.at[o, i],
                device_id=(o2 * inner + j, head),
                device_id_type=MESH,
            ).start()

    loop(0, o, lambda o2: signal(ready.at[o], o2, j, head))

    def piece(ref, src, i, o2, j2, h2, sem):
        pltpu.make_async_remote_copy(
            src_ref=ref.at[:, columns(h2)],
            dst_ref=kvd.at[src, i, place],
            send_sem=sem,
            recv_sem=recv.at[src, j],
            device_id=(o2 * inner + j2, h2),
            device_id_type=MESH,
        ).start()

    @pl.when(o >= DD)
    def _():
        for i, ref in enumerate(inputs):
            for h2 in range(first_heads):
                pl.when((j > 0) | (head != h2))(
                    lambda: piece(ref, o, i, 0, 0, h2, dsent.at[0])
                )

    if LATE:
        loop(0, jnp.minimum(o, 1), zsend)
    else:
        loop(0, o, zsend)
    each_spot((0, j + 1), (0, head + 1), near.at[0])

    def scatter(src, i, ref, first=0, last=8):
        if ABS:
            for t in range(first, min(last, spots)):
                j2, h2 = t // heads, t % heads
                skip = (src >= DD) & (o == 0) if (j2 == 0 and h2 < first_heads) else False
                go = (j2 != j) | (h2 != head)
                if skip is not False:
                    go = go & jnp.logical_not(skip)
                pl.when(go)(lambda: piece(ref, src, i, o, j2, h2, sent.at[src]))
        else:
            group = [(dj, dh) for dj in range(inner) for dh in range(heads)][1:]
            for dj, dh in group:
                j2, h2 = lane(dj), lax.rem(head + dh, heads)
                if DD > 8:
                    piece(ref, src, i, o, j2, h2, sent.at[src])
                else:
                    skip = (src >= DD) & (o == 0) & (j2 == 0) & (h2 < first_heads)
                    pl.when(jnp.logical_not(skip))(lambda: piece(ref, src, i, o, j2, h2, sent.at[src]))

    def upward(o2):
        pl.semaphore_wait(ready.at[o2], 1)
        zsend(o2)

    def own_scatter():
        above = (inner - j) * (heads - head) - 1
        pl.when(above > 0)(lambda: pl.semaphore_wait(near.at[0], above))
        for i, ref in enumerate(inputs):
            scatter(o, i, ref)

    if NEARFIRST:
        own_scatter()
        if LATE:
            loop(1, o, zsend)
        loop(o + 1, outer, upward)
    else:
        loop(o + 1, jnp.minimum(o + 2, outer), upward)
        own_scatter()
        loop(o + 2, outer, upward)

    mine_part = kvd.at[0, :, pl.ds(0, rows)]
    whole = kvd.at[0, :, pl.ds(0, block)]
    part = kvd.at[0, :, pl.ds(0, (heads - 1) * rows)]

    def landed(src, dj):
        ref = whole if dj else part
        pltpu.make_async_copy(ref, ref, recv.at[src, lane(dj)]).wait()

    def arrived(src, i):
        pltpu.make_async_copy(kz.at[0, i], kz.at[0, i], zrecv.at[src, i]).wait()

    def keep(src):
        for i in range(2):
            kvd[src, i, place] = kz[src, i, :, columns(head)]

    def relay(src):
        for i in range(2):
            arrived(src, i)
            scatter(src, i, kz.at[src, i])
        keep(src)

    def relay_pair(near_one, far_one):
        def plain():
            relay(near_one)
            relay(far_one)

        def ranked():
            arrived(near_one, 0)
            scatter(near_one, 0, kz.at[near_one, 0])
            late = [(near_one, 1), (far_one, 0), (far_one, 1)]
            for src, i in late:
                arrived(src, i)
                scatter(src, i, kz.at[src, i], 0, first_heads)
            for src, i in late:
                scatter(src, i, kz.at[src, i], first_heads)
            keep(near_one)
            keep(far_one)

        if PRIO:
            pl.when(o == 0)(ranked)
            pl.when(o > 0)(plain)
        else:
            plain()

    half = max(outer // 2, 1)
    turned = jnp.minimum(o // half, 1)
    seen_from = o + turned * (outer - 1 - 2 * o)

    def source(i):
        a = i + (i + outer - seen_from) // outer
        return a + turned * (outer - 1 - 2 * a)

    lanes = block

    def absorb(blocks, first=False):
        mine = order[seq]
        spots_of = [order[src * inner + l] for src, l in blocks]
        height = len(blocks) * block
        if first:
            row = lax.broadcasted_iota(jnp.int32, (height, lanes), 0)
            col = lax.broadcasted_iota(jnp.int32, (height, lanes), 1)
            start = jnp.full((height, lanes), spots_of[0], jnp.int32) * block
            for l in range(1, len(blocks)):
                start = jnp.where(row >= l * block, (spots_of[l] - l) * block, start)
            mask = mine * block + lax.rem(col, block) >= start + row
        else:
            mask = [jnp.full((1, lanes), spot, jnp.int32) < mine for spot in spots_of]

        def stack(i):
            return jnp.concatenate(
                [kvd[src, i, pl.ds(pl.multiple_of(l * block, block), block)] for src, l in blocks]
            )

        key, value = stack(0), stack(1)
        for g in range(q_heads):
            at = slice(g * block, (g + 1) * block)
            old = None if first else (high[:, at], total[:, at], acc[:, at])
            high[:, at], total[:, at], acc[:, at] = attend(
                q_ref[:, g * HD : (g + 1) * HD], key, value, mask, old
            )

    def both(src):
        for dj in range(inner):
            landed(src, dj)
        return [(src, l) for l in range(inner)]

    qload.wait()
    oload.wait()
    pltpu.make_async_copy(mine_part, mine_part, load_sem.at[0]).wait()
    relayed = outer - 1 if outer <= 8 else 0
    for i in range(relayed - 2):
        relay(source(i))
    if relayed:
        relay_pair(source(relayed - 2), source(relayed - 1))
    absorb(both(o), True)

    def further(i):
        src = source(i)
        if not relayed:
            relay(src)
        absorb(both(src))

    if relayed:
        for i in range(outer - 3):
            further(i)
    else:
        loop(0, outer - 3, further)
    ends = [source(i) for i in range(outer - 3, outer - 1)]
    if not relayed:
        for src in ends:
            relay(src)
    for src in ends:
        landed(src, 0)
    absorb([(src, j) for src in ends])
    for src in ends:
        landed(src, 1)
    absorb([(src, lane(1)) for src in ends])

    def drained(ref, sem):
        pltpu.make_async_copy(ref, ref, sem).wait()

    def pieces(n):
        return kvd.at[0, :, pl.ds(0, n * rows)]

    def drain(src):
        fewer = (src >= DD) & (o == 0)
        if DD < outer:
            for inside in range(2):
                left = spots - 1 - (first_heads - inside)
                pl.when(fewer & (corner == (inside == 1)))(lambda: drained(pieces(left), sent.at[src]))
            pl.when(jnp.logical_not(fewer))(lambda: drained(pieces(spots - 1), sent.at[src]))
        else:
            drained(pieces(spots - 1), sent.at[src])

    if outer > 1:
        drained(kz.at[pl.ds(0, outer - 1)], zsent.at[0])
    if DD < outer:
        pl.when((o >= DD) & jnp.logical_not(corner))(lambda: drained(pieces(first_heads), dsent.at[0]))
        if first_heads > 1:
            pl.when((o >= DD) & corner)(lambda: drained(pieces(first_heads - 1), dsent.at[0]))
    loop(0, outer, drain)


def finish(acc, total, out_ref):
    block, q_cols = out_ref.shape
    for g in range(q_cols // HD):
        lane = slice(g * block, (g + 1) * block)
        part = acc[:, lane] / total[:, lane]
        out_ref[:, g * HD : (g + 1) * HD] = part.T.astype(out_ref.dtype)


def local(devices, heads, queries, keys, values, block_order):
    inner = 2 if devices % 2 == 0 else 1
    outer = devices // inner
    rows, cols = keys.shape
    block, q_cols = queries.shape
    width = cols // heads
    assert width == HD and rows * heads == block
    bf16, f32 = jnp.bfloat16, jnp.float32
    lanes = q_cols // HD * block
    assert inner == 2 and outer >= 3
    acc, total = pl.pallas_call(
        functools.partial(kernel, outer, inner, heads),
        out_shape=(
            pltpu.VMEM((HD, lanes), f32),
            pltpu.VMEM((1, lanes), f32),
        ),
        in_specs=[pl.BlockSpec(memory_space=pltpu.HBM)] * 4,
        out_specs=[pl.BlockSpec(memory_space=pltpu.VMEM)] * 2,
        scratch_shapes=[
            pltpu.SMEM(block_order.shape, jnp.int32),
            pltpu.VMEM((block, q_cols), bf16),
            pltpu.VMEM((outer, 2, rows, cols), bf16),
            pltpu.VMEM((outer, 2, inner * block, width), bf16),
            pltpu.VMEM((1, lanes), f32),
            pltpu.SemaphoreType.DMA((3,)),
            pltpu.SemaphoreType.REGULAR((outer,)),
            pltpu.SemaphoreType.REGULAR((1,)),
            pltpu.SemaphoreType.DMA((1,)),
            pltpu.SemaphoreType.DMA((outer, 2)),
            pltpu.SemaphoreType.DMA((1,)),
            pltpu.SemaphoreType.DMA((outer,)),
            pltpu.SemaphoreType.DMA((outer, inner)),
        ],
        compiler_params=pltpu.CompilerParams(
            collective_id=0, has_side_effects=True, vmem_limit_bytes=67043328 - KB * 1024
        ),
    )(block_order, queries, keys, values)
    return pl.pallas_call(
        finish,
        out_shape=jax.ShapeDtypeStruct((block, q_cols), queries.dtype),
        in_specs=[pl.BlockSpec(memory_space=pltpu.VMEM)] * 2,
        out_specs=pl.BlockSpec(memory_space=pltpu.VMEM),
        compiler_params=pltpu.CompilerParams(vmem_limit_bytes=8 * 1024 * 1024),
    )(acc, total)


def solution(mesh):
    placed = (P("seq", "head"), P(("seq", "head"), None), P(("seq", "head"), None), P())
    return jax.shard_map(
        functools.partial(local, mesh.shape["seq"], mesh.shape["head"]),
        mesh=mesh, in_specs=placed, out_specs=P("seq", "head"), check_vma=False,
    )
```

time: 17.8 us -> 16.9 us (0.949)
  the two profiles are of different devices: /device:TPU:26 before, /device:TPU:0 now
where the time goes in v2:
time: 16.9 us; the launch traced here: 16.8 us
  Pallas kernels  16.8 us (99%)
    pallas_call x1, Pallas kernels, local(): pl.pallas_call(functools.partial(kernel, outer, inner, heads), out_shape=...  15.9 us
    pallas_call x1, Pallas kernels, local(): pl.pallas_call(finish, out_shape=jax.ShapeDtypeStruct((block, q_cols), qu...  0.85 us

profile of v2, /device:TPU:0, one launch (start us, length us, event | category | flops | bytes accessed | tf_op | source)
XLA Modules:
  0.0 16.8 jit_solution(2681679887789633034)
XLA Ops:
  0.0 15.9 %shard_map.46 = (f32[128,1024]{1,0:T(8,128)S(1)}, f32[1,1024]{1,0:T(1,128)S(1)}) custom-call(s32[8]{0:T(128)} %order_hbm.1, bf16[128,1024]{1,0:T(8,128)(2,1)} %q_hbm.1, bf16[32,512]{1,0:T(8,128)(2,1)} %k_hbm.1, bf16[32,512]{1,0:T(8,128)(2,1)} %v_hbm.1), custom_call_target="tpu_custom_call" | custom-call | tf_op jit(solution)/shard_map/pallas_call | solution.py:353
  15.9 0.8 %shard_map.47 = bf16[128,1024]{1,0:T(8,128)(2,1)} custom-call(f32[128,1024]{1,0:T(8,128)S(1)} %get-tuple-element.7.acc, f32[1,1024]{1,0:T(1,128)S(1)} %get-tuple-element.8.total), custom_call_target="tpu_custom_call" | custom-call | tf_op jit(solution)/shard_map/pallas_call | solution.py:380

commit v3 on v2

--- a/solution.py
+++ b/solution.py
@@ -11,9 +11,9 @@
 HD = 128
 NEG = -1e30
 MESH = pl.DeviceIdType.MESH
-DD=9
-ABS=True
 PRIO=True
+SPLITZ=True
+FIN=2
 LATE=True
 KB=600
 NEARFIRST=True
@@ -62,7 +62,7 @@
     o, j = seq // inner, lax.rem(seq, inner)
     first_heads = max(heads // 2, 1)
     spots = inner * heads
-    corner = (j == 0) & (head < first_heads)
+    partner = o + 1 - 2 * lax.rem(o, 2)
     place = pl.ds(pl.multiple_of(j * block + head * rows, rows), rows)
     inputs = (k_hbm, v_hbm)
 
@@ -89,15 +89,6 @@
 
     loop(o + 1, outer, lambda o2: signal(barrier, o2, j, head))
     each_spot((j, inner), (head, heads), barrier)
-
-    @pl.when(corner & (o == 0))
-    def _():
-        def row(o2):
-            for j2 in range(inner):
-                for h2 in range(heads):
-                    pl.when((j2 != j) | (h2 != head))(lambda: signal(barrier, o2, j2, h2))
-
-        loop(DD, outer, row)
 
     own = [
         pltpu.make_async_copy(src.at[:, columns(head)], kvd.at[o, i, place], load_sem.at[0])
@@ -109,20 +100,25 @@
         c.start()
 
     ahead = o + (j + 1) * (head + 1) - 1
-    extra = first_heads - jnp.where(corner, 1, 0)
-    ahead = ahead + jnp.where(o >= DD, extra, 0)
     pl.when(ahead > 0)(lambda: pl.semaphore_wait(barrier, ahead))
 
+    halves = 2 if SPLITZ else 1
+    per_half = heads // halves
+
+    def zpart(f):
+        return pl.ds(f * per_half * width, per_half * width)
+
     def zsend(o2):
-        for i, src in enumerate(inputs):
-            pltpu.make_async_remote_copy(
-                src_ref=src,
-                dst_ref=kz.at[o, i],
-                send_sem=zsent.at[0],
-                recv_sem=zrecv.at[o, i],
-                device_id=(o2 * inner + j, head),
-                device_id_type=MESH,
-            ).start()
+        for f in range(halves):
+            for i, src in enumerate(inputs):
+                pltpu.make_async_remote_copy(
+                    src_ref=src.at[:, zpart(f)],
+                    dst_ref=kz.at[o, i, :, zpart(f)],
+                    send_sem=zsent.at[0],
+                    recv_sem=zrecv.at[o, f, i],
+                    device_id=(o2 * inner + j, head),
+                    device_id_type=MESH,
+                ).start()
 
     loop(0, o, lambda o2: signal(ready.at[o], o2, j, head))
 
@@ -136,38 +132,21 @@
             device_id_type=MESH,
         ).start()
 
-    @pl.when(o >= DD)
-    def _():
-        for i, ref in enumerate(inputs):
-            for h2 in range(first_heads):
-                pl.when((j > 0) | (head != h2))(
-                    lambda: piece(ref, o, i, 0, 0, h2, dsent.at[0])
-                )
-
     if LATE:
         loop(0, jnp.minimum(o, 1), zsend)
     else:
         loop(0, o, zsend)
     each_spot((0, j + 1), (0, head + 1), near.at[0])
 
-    def scatter(src, i, ref, first=0, last=8):
-        if ABS:
-            for t in range(first, min(last, spots)):
-                j2, h2 = t // heads, t % heads
-                skip = (src >= DD) & (o == 0) if (j2 == 0 and h2 < first_heads) else False
-                go = (j2 != j) | (h2 != head)
-                if skip is not False:
-                    go = go & jnp.logical_not(skip)
-                pl.when(go)(lambda: piece(ref, src, i, o, j2, h2, sent.at[src]))
-        else:
-            group = [(dj, dh) for dj in range(inner) for dh in range(heads)][1:]
-            for dj, dh in group:
-                j2, h2 = lane(dj), lax.rem(head + dh, heads)
-                if DD > 8:
-                    piece(ref, src, i, o, j2, h2, sent.at[src])
-                else:
-                    skip = (src >= DD) & (o == 0) & (j2 == 0) & (h2 < first_heads)
-                    pl.when(jnp.logical_not(skip))(lambda: piece(ref, src, i, o, j2, h2, sent.at[src]))
+    def scatter(src, i, ref, targets):
+        for j2, h2 in targets:
+            go = ((j2 != j) | (h2 != head)) & ((j2 == j) | (src != partner))
+            pl.when(go)(lambda: piece(ref, src, i, o, j2, h2, sent.at[0]))
+
+    def places(f, lanes_of=tuple(range(inner))):
+        return [(j2, h2) for j2 in lanes_of for h2 in range(f * per_half, (f + 1) * per_half)]
+
+    every = [(j2, h2) for j2 in range(inner) for h2 in range(heads)]
 
     def upward(o2):
         pl.semaphore_wait(ready.at[o2], 1)
@@ -177,7 +156,7 @@
         above = (inner - j) * (heads - head) - 1
         pl.when(above > 0)(lambda: pl.semaphore_wait(near.at[0], above))
         for i, ref in enumerate(inputs):
-            scatter(o, i, ref)
+            scatter(o, i, ref, every)
 
     if NEARFIRST:
         own_scatter()
@@ -197,41 +176,42 @@
         ref = whole if dj else part
         pltpu.make_async_copy(ref, ref, recv.at[src, lane(dj)]).wait()
 
-    def arrived(src, i):
-        pltpu.make_async_copy(kz.at[0, i], kz.at[0, i], zrecv.at[src, i]).wait()
+    def arrived(src, f, i):
+        ref = kz.at[0, i, :, zpart(f)]
+        pltpu.make_async_copy(ref, ref, zrecv.at[src, f, i]).wait()
 
     def keep(src):
         for i in range(2):
             kvd[src, i, place] = kz[src, i, :, columns(head)]
 
-    def relay(src):
-        for i in range(2):
-            arrived(src, i)
-            scatter(src, i, kz.at[src, i])
-        keep(src)
-
-    def relay_pair(near_one, far_one):
+    def relay(src, parts=tuple(range(2 if SPLITZ else 1))):
+        for f in parts:
+            for i in range(2):
+                arrived(src, f, i)
+                scatter(src, i, kz.at[src, i], places(f))
+
+    def relay_pair(*srcs):
         def plain():
-            relay(near_one)
-            relay(far_one)
+            for src in srcs:
+                relay(src)
 
         def ranked():
-            arrived(near_one, 0)
-            scatter(near_one, 0, kz.at[near_one, 0])
-            late = [(near_one, 1), (far_one, 0), (far_one, 1)]
+            late = [(src, i) for src in srcs for i in range(2)]
             for src, i in late:
-                arrived(src, i)
-                scatter(src, i, kz.at[src, i], 0, first_heads)
+                arrived(src, 0, i)
+                scatter(src, i, kz.at[src, i], places(0, (0,)))
             for src, i in late:
-                scatter(src, i, kz.at[src, i], first_heads)
-            keep(near_one)
-            keep(far_one)
+                scatter(src, i, kz.at[src, i], places(0, tuple(range(1, inner))))
+            for src in srcs:
+                relay(src, tuple(range(1, halves)))
 
         if PRIO:
             pl.when(o == 0)(ranked)
             pl.when(o > 0)(plain)
         else:
             plain()
+        for src in srcs:
+            keep(src)
 
     half = max(outer // 2, 1)
     turned = jnp.minimum(o // half, 1)
@@ -278,17 +258,34 @@
     qload.wait()
     oload.wait()
     pltpu.make_async_copy(mine_part, mine_part, load_sem.at[0]).wait()
+    across = kvd.at[o, :, pl.ds(pl.multiple_of(lane(1) * block, block), block)]
+
+    def hand_over():
+        landed(o, 1)
+        pltpu.make_async_remote_copy(
+            src_ref=across,
+            dst_ref=across,
+            send_sem=dsent.at[0],
+            recv_sem=recv.at[o, lane(1)],
+            device_id=(partner * inner + j, head),
+            device_id_type=MESH,
+        ).start()
+
     relayed = outer - 1 if outer <= 8 else 0
     for i in range(relayed - 2):
         relay(source(i))
+        keep(source(i))
+    hand_over()
     if relayed:
         relay_pair(source(relayed - 2), source(relayed - 1))
-    absorb(both(o), True)
+    landed(o, 0)
+    absorb([(o, l) for l in range(inner)], True)
 
     def further(i):
         src = source(i)
         if not relayed:
             relay(src)
+            keep(src)
         absorb(both(src))
 
     if relayed:
@@ -300,6 +297,7 @@
     if not relayed:
         for src in ends:
             relay(src)
+            keep(src)
     for src in ends:
         landed(src, 0)
     absorb([(src, j) for src in ends])
@@ -310,34 +308,27 @@
     def drained(ref, sem):
         pltpu.make_async_copy(ref, ref, sem).wait()
 
-    def pieces(n):
-        return kvd.at[0, :, pl.ds(0, n * rows)]
-
-    def drain(src):
-        fewer = (src >= DD) & (o == 0)
-        if DD < outer:
-            for inside in range(2):
-                left = spots - 1 - (first_heads - inside)
-                pl.when(fewer & (corner == (inside == 1)))(lambda: drained(pieces(left), sent.at[src]))
-            pl.when(jnp.logical_not(fewer))(lambda: drained(pieces(spots - 1), sent.at[src]))
-        else:
-            drained(pieces(spots - 1), sent.at[src])
-
-    if outer > 1:
-        drained(kz.at[pl.ds(0, outer - 1)], zsent.at[0])
-    if DD < outer:
-        pl.when((o >= DD) & jnp.logical_not(corner))(lambda: drained(pieces(first_heads), dsent.at[0]))
-        if first_heads > 1:
-            pl.when((o >= DD) & corner)(lambda: drained(pieces(first_heads - 1), dsent.at[0]))
-    loop(0, outer, drain)
-
-
-def finish(acc, total, out_ref):
-    block, q_cols = out_ref.shape
-    for g in range(q_cols // HD):
-        lane = slice(g * block, (g + 1) * block)
-        part = acc[:, lane] / total[:, lane]
-        out_ref[:, g * HD : (g + 1) * HD] = part.T.astype(out_ref.dtype)
+    drained(kz.at[pl.ds(0, outer - 1)], zsent.at[0])
+    drained(whole, dsent.at[0])
+    scattered = outer * (spots - 1) - (spots - heads)
+    drained(kvd.at[:, :, pl.ds(0, scattered * rows // outer)], sent.at[0])
+
+
+def finish(acc, total, out_hbm, out, sem):
+    block, q_cols = out.shape
+    count = sem.shape[0]
+    wide = q_cols // count
+    copies = []
+    for n in range(count):
+        for g in range(n * wide // HD, (n + 1) * wide // HD):
+            lane = slice(g * block, (g + 1) * block)
+            part = acc[:, lane] * (1.0 / total[:, lane])
+            out[:, g * HD : (g + 1) * HD] = part.astype(out.dtype).T
+        at = pl.ds(n * wide, wide)
+        copies.append(pltpu.make_async_copy(out.at[:, at], out_hbm.at[:, at], sem.at[n]))
+        copies[-1].start()
+    for copy in copies:
+        copy.wait()
 
 
 def local(devices, heads, queries, keys, values, block_order):
@@ -368,9 +359,9 @@
             pltpu.SemaphoreType.REGULAR((outer,)),
             pltpu.SemaphoreType.REGULAR((1,)),
             pltpu.SemaphoreType.DMA((1,)),
-            pltpu.SemaphoreType.DMA((outer, 2)),
+            pltpu.SemaphoreType.DMA((outer, 2 if SPLITZ else 1, 2)),
             pltpu.SemaphoreType.DMA((1,)),
-            pltpu.SemaphoreType.DMA((outer,)),
+            pltpu.SemaphoreType.DMA((1,)),
             pltpu.SemaphoreType.DMA((outer, inner)),
         ],
         compiler_params=pltpu.CompilerParams(
@@ -381,7 +372,11 @@
         finish,
         out_shape=jax.ShapeDtypeStruct((block, q_cols), queries.dtype),
         in_specs=[pl.BlockSpec(memory_space=pltpu.VMEM)] * 2,
-        out_specs=pl.BlockSpec(memory_space=pltpu.VMEM),
+        out_specs=pl.BlockSpec(memory_space=pltpu.HBM),
+        scratch_shapes=[
+            pltpu.VMEM((block, q_cols), queries.dtype),
+            pltpu.SemaphoreType.DMA((FIN,)),
+        ],
         compiler_params=pltpu.CompilerParams(vmem_limit_bytes=8 * 1024 * 1024),
     )(acc, total)
 

time: 16.9 us -> 16.2 us (0.959)
  the two profiles are of different devices: /device:TPU:0 before, /device:TPU:27 now
where the time goes in v3:
time: 16.2 us; the launch traced here: 16.1 us
  Pallas kernels  16.1 us (99%)
    pallas_call x1, Pallas kernels, local(): pl.pallas_call(functools.partial(kernel, outer, inner, heads), out_shape=...  15.3 us
    pallas_call x1, Pallas kernels, local(): pl.pallas_call(finish, out_shape=jax.ShapeDtypeStruct((block, q_cols), qu...  0.82 us

profile of v3, /device:TPU:27, one launch (start us, length us, event | category | flops | bytes accessed | tf_op | source)
XLA Modules:
  0.0 16.1 jit_solution(6220802039869967936)
XLA Ops:
  0.0 15.3 %shard_map.46 = (f32[128,1024]{1,0:T(8,128)S(1)}, f32[1,1024]{1,0:T(1,128)S(1)}) custom-call(s32[8]{0:T(128)} %order_hbm.1, bf16[128,1024]{1,0:T(8,128)(2,1)} %q_hbm.1, bf16[32,512]{1,0:T(8,128)(2,1)} %k_hbm.1, bf16[32,512]{1,0:T(8,128)(2,1)} %v_hbm.1), custom_call_target="tpu_custom_call" | custom-call | tf_op jit(solution)/shard_map/pallas_call | solution.py:344
  15.3 0.8 %shard_map.47 = bf16[128,1024]{1,0:T(8,128)(2,1)} custom-call(f32[128,1024]{1,0:T(8,128)S(1)} %get-tuple-element.7.acc, f32[1,1024]{1,0:T(1,128)S(1)} %get-tuple-element.8.total), custom_call_target="tpu_custom_call" | custom-call | tf_op jit(solution)/shard_map/pallas_call | solution.py:371

commit v4 on v3

--- a/solution.py
+++ b/solution.py
@@ -14,6 +14,7 @@
 PRIO=True
 SPLITZ=True
 FIN=2
+MODE=0
 LATE=True
 KB=600
 NEARFIRST=True
@@ -298,12 +299,21 @@
         for src in ends:
             relay(src)
             keep(src)
-    for src in ends:
-        landed(src, 0)
-    absorb([(src, j) for src in ends])
-    for src in ends:
-        landed(src, 1)
-    absorb([(src, lane(1)) for src in ends])
+    front = 1 - jnp.minimum(o, 1)
+    if MODE == 1:
+        front = front * 0
+    if MODE == 2:
+        front = front * 0 + 1
+    near_one, far_one = ends
+    landed(near_one, 0)
+    pl.when(front == 1)(lambda: landed(far_one, 0))
+    pl.when(front == 0)(lambda: landed(near_one, 1))
+    turn = front * (far_one - near_one)
+    absorb([(near_one, j), (near_one + turn, lane(1) + front * (j - lane(1)))])
+    pl.when(front == 1)(lambda: landed(near_one, 1))
+    pl.when(front == 0)(lambda: landed(far_one, 0))
+    landed(far_one, 1)
+    absorb([(far_one - turn, j + front * (lane(1) - j)), (far_one, lane(1))])
 
     def drained(ref, sem):
         pltpu.make_async_copy(ref, ref, sem).wait()

time: 16.2 us -> 16 us (0.988)
  the two profiles are of different devices: /device:TPU:27 before, /device:TPU:0 now
where the time goes in v4:
time: 16 us; the launch traced here: 15.7 us
  Pallas kernels  15.7 us (98%)
    pallas_call x1, Pallas kernels, local(): pl.pallas_call(functools.partial(kernel, outer, inner, heads), out_shape=...  14.9 us
    pallas_call x1, Pallas kernels, local(): pl.pallas_call(finish, out_shape=jax.ShapeDtypeStruct((block, q_cols), qu...  0.82 us

profile of v4, /device:TPU:0, one launch (start us, length us, event | category | flops | bytes accessed | tf_op | source)
XLA Modules:
  0.0 15.7 jit_solution(8495923773283479803)
XLA Ops:
  0.0 14.9 %shard_map.46 = (f32[128,1024]{1,0:T(8,128)S(1)}, f32[1,1024]{1,0:T(1,128)S(1)}) custom-call(s32[8]{0:T(128)} %order_hbm.1, bf16[128,1024]{1,0:T(8,128)(2,1)} %q_hbm.1, bf16[32,512]{1,0:T(8,128)(2,1)} %k_hbm.1, bf16[32,512]{1,0:T(8,128)(2,1)} %v_hbm.1), custom_call_target="tpu_custom_call" | custom-call | tf_op jit(solution)/shard_map/pallas_call | solution.py:354
  14.9 0.8 %shard_map.47 = bf16[128,1024]{1,0:T(8,128)(2,1)} custom-call(f32[128,1024]{1,0:T(8,128)S(1)} %get-tuple-element.7.acc, f32[1,1024]{1,0:T(1,128)S(1)} %get-tuple-element.8.total), custom_call_target="tpu_custom_call" | custom-call | tf_op jit(solution)/shard_map/pallas_call | solution.py:381

commit v5 on v4

--- a/solution.py
+++ b/solution.py
@@ -11,13 +11,8 @@
 HD = 128
 NEG = -1e30
 MESH = pl.DeviceIdType.MESH
-PRIO=True
-SPLITZ=True
-FIN=2
-MODE=0
-LATE=True
-KB=600
-NEARFIRST=True
+HALVES = 2
+CHUNKS = 2
 
 
 FACTOR = math.log2(math.e) / math.sqrt(HD)
@@ -53,7 +48,7 @@
     outer, inner, heads,
     order_hbm, q_hbm, k_hbm, v_hbm, acc, total,
     order, q_ref, kz, kvd, high,
-    load_sem, ready, near, zsent, zrecv, dsent, sent, recv,
+    load_sem, ready, near, zsent, zrecv, sent, recv,
 ):
     rows, cols = k_hbm.shape
     block = q_ref.shape[0]
@@ -63,7 +58,6 @@
     o, j = seq // inner, lax.rem(seq, inner)
     first_heads = max(heads // 2, 1)
     spots = inner * heads
-    partner = o + 1 - 2 * lax.rem(o, 2)
     place = pl.ds(pl.multiple_of(j * block + head * rows, rows), rows)
     inputs = (k_hbm, v_hbm)
 
@@ -103,7 +97,7 @@
     ahead = o + (j + 1) * (head + 1) - 1
     pl.when(ahead > 0)(lambda: pl.semaphore_wait(barrier, ahead))
 
-    halves = 2 if SPLITZ else 1
+    halves = HALVES
     per_half = heads // halves
 
     def zpart(f):
@@ -133,15 +127,12 @@
             device_id_type=MESH,
         ).start()
 
-    if LATE:
-        loop(0, jnp.minimum(o, 1), zsend)
-    else:
-        loop(0, o, zsend)
+    loop(0, jnp.minimum(o, 1), zsend)
     each_spot((0, j + 1), (0, head + 1), near.at[0])
 
     def scatter(src, i, ref, targets):
         for j2, h2 in targets:
-            go = ((j2 != j) | (h2 != head)) & ((j2 == j) | (src != partner))
+            go = (j2 != j) | (h2 != head)
             pl.when(go)(lambda: piece(ref, src, i, o, j2, h2, sent.at[0]))
 
     def places(f, lanes_of=tuple(range(inner))):
@@ -159,15 +150,9 @@
         for i, ref in enumerate(inputs):
             scatter(o, i, ref, every)
 
-    if NEARFIRST:
-        own_scatter()
-        if LATE:
-            loop(1, o, zsend)
-        loop(o + 1, outer, upward)
-    else:
-        loop(o + 1, jnp.minimum(o + 2, outer), upward)
-        own_scatter()
-        loop(o + 2, outer, upward)
+    loop(1, o, zsend)
+    own_scatter()
+    loop(o + 1, outer, upward)
 
     mine_part = kvd.at[0, :, pl.ds(0, rows)]
     whole = kvd.at[0, :, pl.ds(0, block)]
@@ -185,32 +170,21 @@
         for i in range(2):
             kvd[src, i, place] = kz[src, i, :, columns(head)]
 
-    def relay(src, parts=tuple(range(2 if SPLITZ else 1))):
+    def relay(src, parts=tuple(range(HALVES))):
         for f in parts:
             for i in range(2):
                 arrived(src, f, i)
                 scatter(src, i, kz.at[src, i], places(f))
 
     def relay_pair(*srcs):
-        def plain():
-            for src in srcs:
-                relay(src)
-
-        def ranked():
-            late = [(src, i) for src in srcs for i in range(2)]
-            for src, i in late:
-                arrived(src, 0, i)
-                scatter(src, i, kz.at[src, i], places(0, (0,)))
-            for src, i in late:
-                scatter(src, i, kz.at[src, i], places(0, tuple(range(1, inner))))
-            for src in srcs:
-                relay(src, tuple(range(1, halves)))
-
-        if PRIO:
-            pl.when(o == 0)(ranked)
-            pl.when(o > 0)(plain)
-        else:
-            plain()
+        late = [(src, i) for src in srcs for i in range(2)]
+        for src, i in late:
+            arrived(src, 0, i)
+            scatter(src, i, kz.at[src, i], places(0, (0,)))
+        for src, i in late:
+            scatter(src, i, kz.at[src, i], places(0, tuple(range(1, inner))))
+        for src in srcs:
+            relay(src, tuple(range(1, halves)))
         for src in srcs:
             keep(src)
 
@@ -259,28 +233,13 @@
     qload.wait()
     oload.wait()
     pltpu.make_async_copy(mine_part, mine_part, load_sem.at[0]).wait()
-    across = kvd.at[o, :, pl.ds(pl.multiple_of(lane(1) * block, block), block)]
-
-    def hand_over():
-        landed(o, 1)
-        pltpu.make_async_remote_copy(
-            src_ref=across,
-            dst_ref=across,
-            send_sem=dsent.at[0],
-            recv_sem=recv.at[o, lane(1)],
-            device_id=(partner * inner + j, head),
-            device_id_type=MESH,
-        ).start()
-
     relayed = outer - 1 if outer <= 8 else 0
     for i in range(relayed - 2):
         relay(source(i))
         keep(source(i))
-    hand_over()
     if relayed:
         relay_pair(source(relayed - 2), source(relayed - 1))
-    landed(o, 0)
-    absorb([(o, l) for l in range(inner)], True)
+    absorb(both(o), True)
 
     def further(i):
         src = source(i)
@@ -300,10 +259,6 @@
             relay(src)
             keep(src)
     front = 1 - jnp.minimum(o, 1)
-    if MODE == 1:
-        front = front * 0
-    if MODE == 2:
-        front = front * 0 + 1
     near_one, far_one = ends
     landed(near_one, 0)
     pl.when(front == 1)(lambda: landed(far_one, 0))
@@ -319,8 +274,7 @@
         pltpu.make_async_copy(ref, ref, sem).wait()
 
     drained(kz.at[pl.ds(0, outer - 1)], zsent.at[0])
-    drained(whole, dsent.at[0])
-    scattered = outer * (spots - 1) - (spots - heads)
+    scattered = outer * (spots - 1)
     drained(kvd.at[:, :, pl.ds(0, scattered * rows // outer)], sent.at[0])
 
 
@@ -369,13 +323,12 @@
             pltpu.SemaphoreType.REGULAR((outer,)),
             pltpu.SemaphoreType.REGULAR((1,)),
             pltpu.SemaphoreType.DMA((1,)),
-            pltpu.SemaphoreType.DMA((outer, 2 if SPLITZ else 1, 2)),
-            pltpu.SemaphoreType.DMA((1,)),
+            pltpu.SemaphoreType.DMA((outer, HALVES, 2)),
             pltpu.SemaphoreType.DMA((1,)),
             pltpu.SemaphoreType.DMA((outer, inner)),
         ],
         compiler_params=pltpu.CompilerParams(
-            collective_id=0, has_side_effects=True, vmem_limit_bytes=67043328 - KB * 1024
+            collective_id=0, has_side_effects=True, vmem_limit_bytes=67043328 - 600 * 1024
         ),
     )(block_order, queries, keys, values)
     return pl.pallas_call(
@@ -385,7 +338,7 @@
         out_specs=pl.BlockSpec(memory_space=pltpu.HBM),
         scratch_shapes=[
             pltpu.VMEM((block, q_cols), queries.dtype),
-            pltpu.SemaphoreType.DMA((FIN,)),
+            pltpu.SemaphoreType.DMA((CHUNKS,)),
         ],
         compiler_params=pltpu.CompilerParams(vmem_limit_bytes=8 * 1024 * 1024),
     )(acc, total)

time: 16 us -> 15.8 us (0.988); the launches traced: 15.7 us -> 15.7 us
  no operation moved by 1% of the time
where the time goes in v5:
time: 15.8 us; the launch traced here: 15.7 us
  Pallas kernels  15.7 us (99%)
    pallas_call x1, Pallas kernels, local(): pl.pallas_call(functools.partial(kernel, outer, inner, heads), out_shape=...  14.9 us
    pallas_call x1, Pallas kernels, local(): pl.pallas_call(finish, out_shape=jax.ShapeDtypeStruct((block, q_cols), qu...  0.82 us

profile of v5, /device:TPU:0, one launch (start us, length us, event | category | flops | bytes accessed | tf_op | source)
XLA Modules:
  0.0 15.7 jit_solution(8830185471945395752)
XLA Ops:
  0.0 14.9 %shard_map.46 = (f32[128,1024]{1,0:T(8,128)S(1)}, f32[1,1024]{1,0:T(1,128)S(1)}) custom-call(s32[8]{0:T(128)} %order_hbm.1, bf16[128,1024]{1,0:T(8,128)(2,1)} %q_hbm.1, bf16[32,512]{1,0:T(8,128)(2,1)} %k_hbm.1, bf16[32,512]{1,0:T(8,128)(2,1)} %v_hbm.1), custom_call_target="tpu_custom_call" | custom-call | tf_op jit(solution)/shard_map/pallas_call | solution.py:308
  14.9 0.8 %shard_map.47 = bf16[128,1024]{1,0:T(8,128)(2,1)} custom-call(f32[128,1024]{1,0:T(8,128)S(1)} %get-tuple-element.7.acc, f32[1,1024]{1,0:T(1,128)S(1)} %get-tuple-element.8.total), custom_call_target="tpu_custom_call" | custom-call | tf_op jit(solution)/shard_map/pallas_call | solution.py:334

commit v6 on v5

--- a/solution.py
+++ b/solution.py
@@ -11,7 +11,6 @@
 HD = 128
 NEG = -1e30
 MESH = pl.DeviceIdType.MESH
-HALVES = 2
 CHUNKS = 2
 
 
@@ -97,23 +96,26 @@
     ahead = o + (j + 1) * (head + 1) - 1
     pl.when(ahead > 0)(lambda: pl.semaphore_wait(barrier, ahead))
 
-    halves = HALVES
-    per_half = heads // halves
-
-    def zpart(f):
-        return pl.ds(f * per_half * width, per_half * width)
+    pair = max(heads // 2, 1)
+
+    def zpart(f, size):
+        return pl.ds(f * width, size * width)
 
     def zsend(o2):
-        for f in range(halves):
-            for i, src in enumerate(inputs):
-                pltpu.make_async_remote_copy(
-                    src_ref=src.at[:, zpart(f)],
-                    dst_ref=kz.at[o, i, :, zpart(f)],
-                    send_sem=zsent.at[0],
-                    recv_sem=zrecv.at[o, f, i],
-                    device_id=(o2 * inner + j, head),
-                    device_id_type=MESH,
-                ).start()
+        def parts(size):
+            for f in range(0, heads, size):
+                for i, src in enumerate(inputs):
+                    pltpu.make_async_remote_copy(
+                        src_ref=src.at[:, zpart(f, size)],
+                        dst_ref=kz.at[o, i, :, zpart(f, size)],
+                        send_sem=zsent.at[0],
+                        recv_sem=zrecv.at[o, f if size == 1 else f + i],
+                        device_id=(o2 * inner + j, head),
+                        device_id_type=MESH,
+                    ).start()
+
+        pl.when(o2 == 0)(lambda: parts(1))
+        pl.when(o2 > 0)(lambda: parts(pair))
 
     loop(0, o, lambda o2: signal(ready.at[o], o2, j, head))
 
@@ -135,8 +137,8 @@
             go = (j2 != j) | (h2 != head)
             pl.when(go)(lambda: piece(ref, src, i, o, j2, h2, sent.at[0]))
 
-    def places(f, lanes_of=tuple(range(inner))):
-        return [(j2, h2) for j2 in lanes_of for h2 in range(f * per_half, (f + 1) * per_half)]
+    def places(f, size, lanes_of=tuple(range(inner))):
+        return [(j2, h2) for j2 in lanes_of for h2 in range(f, f + size)]
 
     every = [(j2, h2) for j2 in range(inner) for h2 in range(heads)]
 
@@ -162,29 +164,43 @@
         ref = whole if dj else part
         pltpu.make_async_copy(ref, ref, recv.at[src, lane(dj)]).wait()
 
-    def arrived(src, f, i):
-        ref = kz.at[0, i, :, zpart(f)]
-        pltpu.make_async_copy(ref, ref, zrecv.at[src, f, i]).wait()
+    def arrived(src, f, i, size):
+        if size > 1:
+            ref = kz.at[0, i, :, zpart(f, size)]
+            pltpu.make_async_copy(ref, ref, zrecv.at[src, f + i]).wait()
+        elif i == 0:
+            ref = kz.at[0, :, :, zpart(f, size)]
+            pltpu.make_async_copy(ref, ref, zrecv.at[src, f]).wait()
+
+    def by_plane(body):
+        pl.when(o == 0)(lambda: body(1))
+        pl.when(o > 0)(lambda: body(pair))
 
     def keep(src):
         for i in range(2):
             kvd[src, i, place] = kz[src, i, :, columns(head)]
 
-    def relay(src, parts=tuple(range(HALVES))):
-        for f in parts:
+    def pass_on(src, first, size):
+        for f in range(first, heads, size):
             for i in range(2):
-                arrived(src, f, i)
-                scatter(src, i, kz.at[src, i], places(f))
+                arrived(src, f, i, size)
+                scatter(src, i, kz.at[src, i], places(f, size))
+
+    def relay(src):
+        by_plane(lambda size: pass_on(src, 0, size))
 
     def relay_pair(*srcs):
-        late = [(src, i) for src in srcs for i in range(2)]
-        for src, i in late:
-            arrived(src, 0, i)
-            scatter(src, i, kz.at[src, i], places(0, (0,)))
-        for src, i in late:
-            scatter(src, i, kz.at[src, i], places(0, tuple(range(1, inner))))
-        for src in srcs:
-            relay(src, tuple(range(1, halves)))
+        def serve(size):
+            late = [(src, f, i) for f in range(0, pair, size) for src in srcs for i in range(2)]
+            for src, f, i in late:
+                arrived(src, f, i, size)
+                scatter(src, i, kz.at[src, i], places(f, size, (0,)))
+            for src, f, i in late:
+                scatter(src, i, kz.at[src, i], places(f, size, tuple(range(1, inner))))
+            for src in srcs:
+                pass_on(src, pair, size)
+
+        by_plane(serve)
         for src in srcs:
             keep(src)
 
@@ -304,7 +320,7 @@
     assert width == HD and rows * heads == block
     bf16, f32 = jnp.bfloat16, jnp.float32
     lanes = q_cols // HD * block
-    assert inner == 2 and outer >= 3
+    assert inner == 2 and outer >= 3 and heads >= 4
     acc, total = pl.pallas_call(
         functools.partial(kernel, outer, inner, heads),
         out_shape=(
@@ -323,7 +339,7 @@
             pltpu.SemaphoreType.REGULAR((outer,)),
             pltpu.SemaphoreType.REGULAR((1,)),
             pltpu.SemaphoreType.DMA((1,)),
-            pltpu.SemaphoreType.DMA((outer, HALVES, 2)),
+            pltpu.SemaphoreType.DMA((outer, heads)),
             pltpu.SemaphoreType.DMA((1,)),
             pltpu.SemaphoreType.DMA((outer, inner)),
         ],

time: 15.8 us -> 15.7 us (level)
  the two profiles are of different devices: /device:TPU:0 before, /device:TPU:25 now
where the time goes in v6:
time: 15.7 us; the launch traced here: 15.5 us
  Pallas kernels  15.5 us (99%)
    pallas_call x1, Pallas kernels, local(): pl.pallas_call(functools.partial(kernel, outer, inner, heads), out_shape=...  14.7 us
    pallas_call x1, Pallas kernels, local(): pl.pallas_call(finish, out_shape=jax.ShapeDtypeStruct((block, q_cols), qu...  0.82 us

profile of v6, /device:TPU:25, one launch (start us, length us, event | category | flops | bytes accessed | tf_op | source)
XLA Modules:
  0.0 15.5 jit_solution(2182839755995782232)
XLA Ops:
  0.0 14.7 %shard_map.46 = (f32[128,1024]{1,0:T(8,128)S(1)}, f32[1,1024]{1,0:T(1,128)S(1)}) custom-call(s32[8]{0:T(128)} %order_hbm.1, bf16[128,1024]{1,0:T(8,128)(2,1)} %q_hbm.1, bf16[32,512]{1,0:T(8,128)(2,1)} %k_hbm.1, bf16[32,512]{1,0:T(8,128)(2,1)} %v_hbm.1), custom_call_target="tpu_custom_call" | custom-call | tf_op jit(solution)/shard_map/pallas_call | solution.py:324
  14.7 0.8 %shard_map.47 = bf16[128,1024]{1,0:T(8,128)(2,1)} custom-call(f32[128,1024]{1,0:T(8,128)S(1)} %get-tuple-element.7.acc, f32[1,1024]{1,0:T(1,128)S(1)} %get-tuple-element.8.total), custom_call_target="tpu_custom_call" | custom-call | tf_op jit(solution)/shard_map/pallas_call | solution.py:350
